TPU v7x, 256 devices: a whole 4x4x8 slice. The times are simulated.
256 devices in a mesh: vx: 16 (over y, x), vy: 16 (over z, core).
Axes of the slice: x: 4, y: 4, z: 8, core: 2. Of those that a mesh axis runs over, the one named last changes fastest.
Arguments:
- hidden: bfloat16 [1024, 5120], P(('vx', 'vy')), may hold values from -96 to 96
- unembed: bfloat16 [152064, 5120], P(('vx', 'vy')), may hold values from -2 to 2
- loss_mask: int32 [1024], P(('vx', 'vy')), may hold values 0 or 1
- seq_ids: int32 [1024], P(('vx', 'vy')), may hold values from 0 to 7, never falling along the last dimension, each value on 1 to 256 neighbouring positions
Outputs:
- entropy: float32 [1024], P(('vx', 'vy'))
- seq_mean: float32 [8], replicated
Inputs may be any that keep to these rules, and one draw needn't show every extreme that they name: `seq_ids`: sequence numbers never fall along the tokens; each sequence has 1 to 256 tokens.
All inputs are finite; a program needn't handle non-finite values. No bound on the sum of `loss_mask` on one device may be relied on, other than what follows from the above.
Results may differ from a plain program's by a relative error of at most 0.0013.
Values may be sent and summed in bfloat16 or wider, within the bound.
No kernel may reach another device: no remote copies, remote signals or barrier semaphores. Data moves between devices by JAX's collectives and lax.ppermute only.
A program may use at most 128 MiB of HBM per device.

v0:
```python
import functools

import jax
import jax.numpy as jnp
from jax import lax
from jax.experimental import pallas as pl
from jax.experimental.pallas import tpu as pltpu
from jax.sharding import Mesh
from jax.sharding import PartitionSpec as P


SEQS = 8
NY, NX, NZ, NC = 4, 4, 8, 2
ALL = ("y", "x", "z", "c")
LANES = 128
CHUNK = 600


def rank_of(y, x, z, c):
    return (((y % NY) * NX + x % NX) * NZ + z % NZ) * NC + c


def pairs(where):
    return [
        (rank_of(y, x, z, c), rank_of(*where(y, x, z, c)))
        for y in range(NY)
        for x in range(NX)
        for z in range(NZ)
        for c in range(NC)
    ]


def moved(value, where):
    return lax.ppermute(value, ALL, pairs(where))


def joined_rows(*parts):
    return jnp.concatenate(parts, axis=0)


def other_core(y, x, z, c):
    return (y, x, z, 1 - c)


def along_near(step):
    return lambda y, x, z, c: (y + step, x, z, c) if c == 0 else (y, x + step, z, c)


def along_far(step):
    return lambda y, x, z, c: (y, x + step, z, c) if c == 0 else (y + step, x, z, c)


def copy_for_each(shard, axis):
    copies = jnp.broadcast_to(shard, (lax.axis_size(axis), *shard.shape))
    return lax.all_to_all(copies, axis, split_axis=0, concat_axis=0, tiled=True)


def gathered(hidden):
    line = copy_for_each(hidden, "z").reshape(-1, hidden.shape[1])
    one = moved(line, along_near(-1))
    three = moved(line, along_near(1))
    two = moved(line, along_near(2))
    first = joined_rows(line, one)
    second = joined_rows(two, three)
    first_1 = moved(first, along_far(-1))
    second_3 = moved(second, along_far(1))
    second_1 = moved(second, along_far(-1))
    first_3 = moved(first, along_far(1))
    first_2 = moved(first_1, along_far(-1))
    second_2 = moved(second_3, along_far(1))
    return (first, second, first_1, second_3), (first_3, second_1, first_2, second_2)


EARLY = ((0, 0, 64), (1, 0, 64), (2, 0, 64), (3, 0, 64))
LATE = ((0, 0, 64), (1, 0, 64), (2, 0, 64), (3, 0, 64))


def piece_stats(heads, pieces, order, copies=(None, None)):
    depth = heads[0].shape[1]
    whole = jnp.concatenate([pieces[k][start:stop, :] for k, start, stop in order], axis=0)
    rows, notes = whole[:, :depth], whole[:, depth:]
    found = []
    for head, copy in zip(heads, copies):
        if copy is not None:
            copy.wait()
        for start in range(0, head.shape[0], CHUNK):
            stop = min(start + CHUNK, head.shape[0])
            logits = lax.dot_general(
                head[start:stop, :], rows, (((1,), (1,)), ((), ())), preferred_element_type=jnp.float32
            )
            peak = jnp.max(logits, axis=0, keepdims=True)
            shifted = logits - peak
            weight = jnp.exp(shifted)
            norm = jnp.sum(weight, axis=0, keepdims=True)
            tilt = jnp.sum(weight * shifted, axis=0, keepdims=True)
            found.append((peak, norm, tilt))
    peak = functools.reduce(jnp.maximum, [f[0] for f in found])
    norm, tilt = jnp.zeros_like(peak), jnp.zeros_like(peak)
    for p, n, t in found:
        shift = p - peak
        scale = jnp.exp(shift)
        norm += scale * n
        tilt += scale * (t + shift * n)
    picks = lax.broadcasted_iota(jnp.int32, (8, LANES), 0) == lax.broadcasted_iota(jnp.int32, (8, LANES), 1)
    marks = lax.dot_general(
        picks.astype(jnp.bfloat16), notes, (((1,), (1,)), ((), ())), preferred_element_type=jnp.float32
    )
    log_norm = jnp.log(norm)
    return jnp.concatenate([peak + log_norm, log_norm - tilt / norm, marks[:6]], axis=0)


def early_kernel(w0, w1, *refs):
    pieces, (out, v0, v1, sems) = refs[:-4], refs[-4:]
    copies = [pltpu.make_async_copy(w, v, sems.at[k]) for k, (w, v) in enumerate(((w0, v0), (w1, v1)))]
    for copy in copies:
        copy.start()
    out[...] = piece_stats((v0, v1), pieces, EARLY, copies)


def late_kernel(place, w0, w1, early, *refs):
    late = piece_stats((w0, w1), refs[:-1], LATE)
    out = refs[-1]
    far, near = place[0], place[1]
    low = lax.broadcasted_iota(jnp.int32, (8, LANES), 1) < LANES // 2
    a0, a1 = early[:, :LANES], early[:, LANES:]
    b0, b1 = late[:, :LANES], late[:, LANES:]
    turned = [a0, jnp.where(low, a1, b0), b1, jnp.where(low, b0, a1)]
    turned = [pltpu.roll(t, near * (LANES // 4), 1) for t in turned]
    for row in range(4):
        value = turned[row]
        for step in range(1, 4):
            value = jnp.where(far == step, turned[(row - step) % 4], value)
        for kind in range(4):
            out[4 * kind + row : 4 * kind + row + 1, :] = value[kind : kind + 1]


def joined(parts):
    level, spread = parts[:, :4], parts[:, 4:]
    top = jnp.max(level, axis=0)
    below = top[None] - level
    share = jnp.exp(-below)
    return top, jnp.sum(share, axis=0), jnp.sum(share * (below + spread), axis=0)


def in_vmem(*arrays):
    return [pltpu.with_memory_space_constraint(a, pltpu.VMEM) for a in arrays]


VMEM = pl.BlockSpec(memory_space=pltpu.VMEM)
ANY = pl.BlockSpec(memory_space=pl.ANY)


def cost(heads):
    rows, depth = 2 * heads[0].shape[0], heads[0].shape[1]
    return pl.CostEstimate(
        flops=4 * LANES * rows * depth,
        bytes_accessed=2 * (2 * LANES + rows) * depth,
        transcendentals=2 * LANES * rows,
    )


def early_stats(heads, pieces):
    return pl.pallas_call(
        early_kernel,
        out_shape=(
            jax.ShapeDtypeStruct((8, 2 * LANES), jnp.float32),
            *[pltpu.VMEM(h.shape, h.dtype) for h in heads],
        ),
        in_specs=[pl.BlockSpec(memory_space=pltpu.HBM)] * 2 + [VMEM] * len(pieces),
        out_specs=[VMEM] * 3,
        scratch_shapes=[pltpu.SemaphoreType.DMA((2,))],
        cost_estimate=cost(heads),
        compiler_params=pltpu.CompilerParams(vmem_limit_bytes=12 << 20),
    )(*[pltpu.with_memory_space_constraint(h, pltpu.HBM) for h in heads], *in_vmem(*pieces))


def late_stats(place, heads, early, pieces):
    return pl.pallas_call(
        late_kernel,
        out_shape=jax.ShapeDtypeStruct((16, LANES), jnp.float32),
        in_specs=[pl.BlockSpec(memory_space=pltpu.SMEM)] + [VMEM] * (3 + len(pieces)),
        out_specs=VMEM,
        cost_estimate=cost(heads),
        compiler_params=pltpu.CompilerParams(vmem_limit_bytes=12 << 20),
    )(place, *in_vmem(*heads, early, *pieces))


def per_device(hidden, unembed, loss_mask, seq_ids):
    y, x, z, c = (lax.axis_index(a) for a in ALL)
    near = jnp.where(c == 0, y, x)
    far = jnp.where(c == 0, x, y)
    heads = (unembed, moved(unembed, other_core))
    lane = lax.broadcasted_iota(jnp.int32, (hidden.shape[0], LANES), 1)
    notes = jnp.where(lane == 0, loss_mask[:, None], jnp.where(lane == 1, seq_ids[:, None], 0))
    early, late = gathered(jnp.concatenate([hidden, notes.astype(hidden.dtype)], axis=1))
    stats, *heads = early_stats(heads, early)
    stats = late_stats(jnp.stack([far, near]), heads, stats, late)
    kinds = jnp.arange(SEQS, dtype=jnp.int32)[:, None, None]
    member = (stats[8:12] > 0)[None] & (stats[12:16].astype(jnp.int32)[None] == kinds)
    member = member.astype(jnp.float32)
    counts = jnp.sum(member, axis=(1, 2))
    at = ((far * 4 + near) * NZ + z) * 4
    mine, member, counts, at = lax.optimization_barrier((stats[:8], member, counts, at))
    top, total, mixed = joined(copy_for_each(mine, "z"))
    log_total = jnp.log(total)
    both = jnp.concatenate([top + log_total, log_total + mixed / total], axis=0)
    top, total, mixed = joined(copy_for_each(both, ("y", "x")))
    entropy_rows = jnp.log(total) + mixed / total
    entropy = lax.dynamic_slice(entropy_rows.reshape(-1), (at,), (4,), allow_negative_indices=False)
    sums = jnp.sum(member * entropy_rows[None], axis=(1, 2))
    both = jnp.stack([sums, counts])
    both = both + moved(both, other_core)
    seq_mean = both[0] / jnp.maximum(both[1], 1.0)
    return (entropy, seq_mean)


def solution(mesh):
    split = Mesh(mesh.devices.reshape(NY, NX, NZ, NC), ALL)

    return jax.shard_map(
        per_device,
        mesh=split,
        in_specs=(P(ALL, None), P(ALL, None), P(ALL), P(ALL)),
        out_specs=(P(ALL), P()),
        check_vma=False,
    )
```

profile of v0, /device:TPU:1, one launch (start us, length us, event | category | flops | bytes accessed | tf_op | source)
XLA Modules:
  0.0 96.9 jit_solution(4182765268904424171)
XLA Ops:
  0.6 3.3 %collective-permute-start = (bf16[594,5120]{1,0:T(8,128)(2,1)}, bf16[594,5120]{1,0:T(8,128)(2,1)}, u32[]{:S(2)}, u32[]{:S(2)}) collective-permute-start(bf16[594,5120]{1,0:T(8,128)(2,1)} %w0.1), channel_id=1, source_target_pairs={{0,1},{1,0},{2,3},{3,2},{4,5},{5,4},{6,7},{7,6},{8,9},{9,8},{10,11... | collective-permute-start | bytes 18247688 | tf_op jit(solution)/shard_map/ppermute | solution.py:34
  3.9 0.7 select_convert_fusion
  4.7 0.8 pad_maximum_fusion
  5.5 0.1 broadcast_in_dim.37
  5.6 20.2 %all_to_all.15 = bf16[8,4,5248]{2,1,0:T(4,128)(2,1)S(1)} all-to-all(bf16[8,4,5248]{2,1,0:T(4,128)(2,1)S(1)} %broadcast_in_dim.37), channel_id=1, replica_groups=mesh['y'=4,'x'=4,'z'=8,'c'=2] {'z'}, dimensions={0} | all-to-all | bytes 671744 | tf_op jit(solution)/shard_map/all_to_all | solution.py:55
  25.8 0.1 reshape.29
  25.9 2.8 %collective-permute-start.2 = (bf16[32,5248]{1,0:T(8,128)(2,1)S(1)}, bf16[32,5248]{1,0:T(8,128)(2,1)S(1)}, u32[]{:S(2)}, u32[]{:S(2)}) collective-permute-start(bf16[32,5248]{1,0:T(8,128)(2,1)S(1)} %reshape.29), channel_id=1, source_target_pairs={{0,128},{1,33},{2,130},{3,35},{4,132},{5,37},{6,134},{7,39},{8,136... | collective-permute-start | bytes 1007624 | tf_op jit(solution)/shard_map/ppermute | solution.py:34
  28.7 0.3 collective-permute-start.3
  29.0 2.4 %collective-permute-start.1 = (bf16[32,5248]{1,0:T(8,128)(2,1)S(1)}, bf16[32,5248]{1,0:T(8,128)(2,1)S(1)}, u32[]{:S(2)}, u32[]{:S(2)}) collective-permute-start(bf16[32,5248]{1,0:T(8,128)(2,1)S(1)} %reshape.29), channel_id=1, source_target_pairs={{0,192},{1,49},{2,194},{3,51},{4,196},{5,53},{6,198},{7,55},{8,200... | collective-permute-start | bytes 1007624 | tf_op jit(solution)/shard_map/ppermute | solution.py:34
  31.5 2.3 %collective-permute-done.2 = bf16[32,5248]{1,0:T(8,128)(2,1)S(1)} collective-permute-done((bf16[32,5248]{1,0:T(8,128)(2,1)S(1)}, bf16[32,5248]{1,0:T(8,128)(2,1)S(1)}, u32[]{:S(2)}, u32[]{:S(2)}) %collective-permute-start.2) | collective-permute-done | bytes 335904 | tf_op jit(solution)/shard_map/ppermute | solution.py:34
  33.8 3.6 %collective-permute-done.3 = bf16[32,5248]{1,0:T(8,128)(2,1)S(1)} collective-permute-done((bf16[32,5248]{1,0:T(8,128)(2,1)S(1)}, bf16[32,5248]{1,0:T(8,128)(2,1)S(1)}, u32[]{:S(2)}, u32[]{:S(2)}) %collective-permute-start.3) | collective-permute-done | bytes 335904 | tf_op jit(solution)/shard_map/ppermute | solution.py:34
  37.4 1.1 %collective-permute-start.5 = (bf16[64,5248]{1,0:T(8,128)(2,1)S(1)}, bf16[64,5248]{1,0:T(8,128)(2,1)S(1)}, u32[]{:S(2)}, u32[]{:S(2)}) collective-permute-start(bf16[64,5248]{1,0:T(8,128)(2,1)S(1)} %constant_dynamic-update-slice_fusion.2.refs_1_), channel_id=1, source_target_pairs={{0,16},{1,65},{2,18},{3,67},{4,20},{5,69},{6,22},{7,71},{8,24},{9,... | collective-permute-start | bytes 2015240 | tf_op jit(solution)/shard_map/ppermute | solution.py:34
  38.5 0.0 collective-permute-done.1
  38.5 1.8 %collective-permute-start.4 = (bf16[64,5248]{1,0:T(8,128)(2,1)S(1)}, bf16[64,5248]{1,0:T(8,128)(2,1)S(1)}, u32[]{:S(2)}, u32[]{:S(2)}) collective-permute-start(bf16[64,5248]{1,0:T(8,128)(2,1)S(1)} %constant_dynamic-update-slice_fusion.refs_0_), channel_id=1, source_target_pairs={{0,48},{1,193},{2,50},{3,195},{4,52},{5,197},{6,54},{7,199},{8,56}... | collective-permute-start | bytes 2015240 | tf_op jit(solution)/shard_map/ppermute | solution.py:34
  40.4 1.4 %collective-permute-start.7 = (bf16[64,5248]{1,0:T(8,128)(2,1)S(1)}, bf16[64,5248]{1,0:T(8,128)(2,1)S(1)}, u32[]{:S(2)}, u32[]{:S(2)}) collective-permute-start(bf16[64,5248]{1,0:T(8,128)(2,1)S(1)} %constant_dynamic-update-slice_fusion.2.refs_1_), channel_id=1, source_target_pairs={{0,48},{1,193},{2,50},{3,195},{4,52},{5,197},{6,54},{7,199},{8,56}... | collective-permute-start | bytes 2015240 | tf_op jit(solution)/shard_map/ppermute | solution.py:34
  41.8 0.0 collective-permute-start.6
  41.8 6.8 %collective-permute-done.5.refs_3_ = bf16[64,5248]{1,0:T(8,128)(2,1)S(1)} collective-permute-done((bf16[64,5248]{1,0:T(8,128)(2,1)S(1)}, bf16[64,5248]{1,0:T(8,128)(2,1)S(1)}, u32[]{:S(2)}, u32[]{:S(2)}) %collective-permute-start.5) | collective-permute-done | bytes 671776 | tf_op jit(solution)/shard_map/ppermute | solution.py:34
  48.7 0.0 collective-permute-start.9
  48.7 0.0 collective-permute-done.4.refs_2_
  48.7 2.9 %collective-permute-start.8 = (bf16[64,5248]{1,0:T(8,128)(2,1)S(1)}, bf16[64,5248]{1,0:T(8,128)(2,1)}, u32[]{:S(2)}, u32[]{:S(2)}) collective-permute-start(bf16[64,5248]{1,0:T(8,128)(2,1)S(1)} %collective-permute-done.4.refs_2_), channel_id=1, source_target_pairs={{0,48},{1,193},{2,50},{3,195},{4,52},{5,197},{6,54},{7,199},{8,56}... | collective-permute-start | bytes 2015240 | tf_op jit(solution)/shard_map/ppermute | solution.py:34
  51.6 0.1 pad_add_fusion.place
  51.6 0.0 collective-permute-done.w1
  51.7 9.9 %shard_map.59 = (f32[8,256]{1,0:T(8,128)S(1)}, bf16[594,5120]{1,0:T(8,128)(2,1)S(1)}, bf16[594,5120]{1,0:T(8,128)(2,1)S(1)}) custom-call(bf16[594,5120]{1,0:T(8,128)(2,1)} %w0.1, bf16[594,5120]{1,0:T(8,128)(2,1)} %collective-permute-done.w1, bf16[64,5248]{1,0:T(8,128)(2,1)S(1)} %constant_dynamic-update-slice_fusion.refs_0_, ...), custom_call_target="tpu_custom_call" | custom-call | flops 3114270720 | bytes 14786560 | tf_op jit(solution)/shard_map/pallas_call | solution.py:163
  61.6 0.0 collective-permute-done.7.refs_1_
  61.6 0.0 collective-permute-done.6.refs_0_
  61.6 1.6 %collective-permute-done.9.refs_3_ = bf16[64,5248]{1,0:T(8,128)(2,1)} collective-permute-done((bf16[64,5248]{1,0:T(8,128)(2,1)S(1)}, bf16[64,5248]{1,0:T(8,128)(2,1)}, u32[]{:S(2)}, u32[]{:S(2)}) %collective-permute-start.9) | collective-permute-done | bytes 671776 | tf_op jit(solution)/shard_map/ppermute | solution.py:34
  63.2 0.0 collective-permute-done.8.refs_2_
  63.2 5.3 %shard_map.60 = f32[16,128]{1,0:T(8,128)S(1)} custom-call(s32[2]{0:T(128)S(1)} %pad_add_fusion.place, bf16[594,5120]{1,0:T(8,128)(2,1)S(1)} %get-tuple-element.9.w0, bf16[594,5120]{1,0:T(8,128)(2,1)S(1)} %get-tuple-element.10.w1, f32[8,256]{1,0:T(8,128)S(1)} %get-tuple-element.11.early, bf16[64,5248]{1,0:T(8,128)(2,1)} %collective-permute-done.6.refs_0_, ...), custom_call_target="tpu_custom_call" | custom-call | flops 3114270720 | bytes 14786560 | tf_op jit(solution)/shard_map/pallas_call | solution.py:178
  68.5 0.1 fusion.8
  68.6 9.3 %all_to_all.16 = f32[8,8,128]{2,1,0:T(8,128)S(1)} all-to-all(f32[8,8,128]{2,1,0:T(8,128)S(1)} %broadcast_in_dim.38), channel_id=1, replica_groups=mesh['y'=4,'x'=4,'z'=8,'c'=2] {'z'}, dimensions={0} | all-to-all | bytes 65536 | tf_op jit(solution)/shard_map/all_to_all | solution.py:55
  78.1 12.5 %all_to_all.17 = f32[16,8,128]{2,1,0:T(8,128)S(1)} all-to-all(f32[16,8,128]{2,1,0:T(8,128)S(1)} %broadcast_in_dim.39), channel_id=1, replica_groups=mesh['y'=4,'x'=4,'z'=8,'c'=2] {'y','x'}, dimensions={0} | all-to-all | bytes 131072 | tf_op jit(solution)/shard_map/all_to_all | solution.py:55
  90.6 0.1 multiply_reduce_fusion
  90.8 4.8 %collective-permute-start.10 = (f32[2,8]{1,0:T(2,128)S(1)}, f32[2,8]{1,0:T(2,128)S(1)}, u32[]{:S(2)}, u32[]{:S(2)}) collective-permute-start(f32[2,8]{1,0:T(2,128)S(1)} %pad_maximum_fusion.2), channel_id=1, source_target_pairs={{0,1},{1,0},{2,3},{3,2},{4,5},{5,4},{6,7},{7,6},{8,9},{9,8},{10,11... | collective-permute-start | bytes 200 | tf_op jit(solution)/shard_map/ppermute | solution.py:34
  95.6 0.6 dynamic_slice.3
  96.2 0.2 collective-permute-done.10
  96.4 0.5 fusion.9
  (20 shorter events, 0.3 us)
Async XLA Ops:
  0.6 51.0 %collective-permute-start = (bf16[594,5120]{1,0:T(8,128)(2,1)}, bf16[594,5120]{1,0:T(8,128)(2,1)}, u32[]{:S(2)}, u32[]{:S(2)}) collective-permute-start(bf16[594,5120]{1,0:T(8,128)(2,1)} %w0.1), channel_id=1, source_target_pairs={{0,1},{1,0},{2,3},{3,2},{4,5},{5,4},{6,7},{7,6},{8,9},{9,8},{10,11... | collective-permute-start | bytes 18247688 | tf_op jit(solution)/shard_map/ppermute | solution.py:34
  25.9 7.9 %collective-permute-start.2 = (bf16[32,5248]{1,0:T(8,128)(2,1)S(1)}, bf16[32,5248]{1,0:T(8,128)(2,1)S(1)}, u32[]{:S(2)}, u32[]{:S(2)}) collective-permute-start(bf16[32,5248]{1,0:T(8,128)(2,1)S(1)} %reshape.29), channel_id=1, source_target_pairs={{0,128},{1,33},{2,130},{3,35},{4,132},{5,37},{6,134},{7,39},{8,136... | collective-permute-start | bytes 1007624 | tf_op jit(solution)/shard_map/ppermute | solution.py:34
  28.7 8.7 %collective-permute-start.3 = (bf16[32,5248]{1,0:T(8,128)(2,1)S(1)}, bf16[32,5248]{1,0:T(8,128)(2,1)S(1)}, u32[]{:S(2)}, u32[]{:S(2)}) collective-permute-start(bf16[32,5248]{1,0:T(8,128)(2,1)S(1)} %reshape.29), channel_id=1, source_target_pairs={{0,64},{1,17},{2,66},{3,19},{4,68},{5,21},{6,70},{7,23},{8,72},{9,... | collective-permute-start | bytes 1007624 | tf_op jit(solution)/shard_map/ppermute | solution.py:34
  29.0 9.4 %collective-permute-start.1 = (bf16[32,5248]{1,0:T(8,128)(2,1)S(1)}, bf16[32,5248]{1,0:T(8,128)(2,1)S(1)}, u32[]{:S(2)}, u32[]{:S(2)}) collective-permute-start(bf16[32,5248]{1,0:T(8,128)(2,1)S(1)} %reshape.29), channel_id=1, source_target_pairs={{0,192},{1,49},{2,194},{3,51},{4,196},{5,53},{6,198},{7,55},{8,200... | collective-permute-start | bytes 1007624 | tf_op jit(solution)/shard_map/ppermute | solution.py:34
  37.4 11.3 %collective-permute-start.5 = (bf16[64,5248]{1,0:T(8,128)(2,1)S(1)}, bf16[64,5248]{1,0:T(8,128)(2,1)S(1)}, u32[]{:S(2)}, u32[]{:S(2)}) collective-permute-start(bf16[64,5248]{1,0:T(8,128)(2,1)S(1)} %constant_dynamic-update-slice_fusion.2.refs_1_), channel_id=1, source_target_pairs={{0,16},{1,65},{2,18},{3,67},{4,20},{5,69},{6,22},{7,71},{8,24},{9,... | collective-permute-start | bytes 2015240 | tf_op jit(solution)/shard_map/ppermute | solution.py:34
  38.5 10.2 %collective-permute-start.4 = (bf16[64,5248]{1,0:T(8,128)(2,1)S(1)}, bf16[64,5248]{1,0:T(8,128)(2,1)S(1)}, u32[]{:S(2)}, u32[]{:S(2)}) collective-permute-start(bf16[64,5248]{1,0:T(8,128)(2,1)S(1)} %constant_dynamic-update-slice_fusion.refs_0_), channel_id=1, source_target_pairs={{0,48},{1,193},{2,50},{3,195},{4,52},{5,197},{6,54},{7,199},{8,56}... | collective-permute-start | bytes 2015240 | tf_op jit(solution)/shard_map/ppermute | solution.py:34
  40.4 21.2 %collective-permute-start.7 = (bf16[64,5248]{1,0:T(8,128)(2,1)S(1)}, bf16[64,5248]{1,0:T(8,128)(2,1)S(1)}, u32[]{:S(2)}, u32[]{:S(2)}) collective-permute-start(bf16[64,5248]{1,0:T(8,128)(2,1)S(1)} %constant_dynamic-update-slice_fusion.2.refs_1_), channel_id=1, source_target_pairs={{0,48},{1,193},{2,50},{3,195},{4,52},{5,197},{6,54},{7,199},{8,56}... | collective-permute-start | bytes 2015240 | tf_op jit(solution)/shard_map/ppermute | solution.py:34
  41.8 19.8 %collective-permute-start.6 = (bf16[64,5248]{1,0:T(8,128)(2,1)S(1)}, bf16[64,5248]{1,0:T(8,128)(2,1)}, u32[]{:S(2)}, u32[]{:S(2)}) collective-permute-start(bf16[64,5248]{1,0:T(8,128)(2,1)S(1)} %constant_dynamic-update-slice_fusion.refs_0_), channel_id=1, source_target_pairs={{0,16},{1,65},{2,18},{3,67},{4,20},{5,69},{6,22},{7,71},{8,24},{9,... | collective-permute-start | bytes 2015240 | tf_op jit(solution)/shard_map/ppermute | solution.py:34
  48.7 14.5 %collective-permute-start.9 = (bf16[64,5248]{1,0:T(8,128)(2,1)S(1)}, bf16[64,5248]{1,0:T(8,128)(2,1)}, u32[]{:S(2)}, u32[]{:S(2)}) collective-permute-start(bf16[64,5248]{1,0:T(8,128)(2,1)S(1)} %collective-permute-done.5.refs_3_), channel_id=1, source_target_pairs={{0,16},{1,65},{2,18},{3,67},{4,20},{5,69},{6,22},{7,71},{8,24},{9,... | collective-permute-start | bytes 2015240 | tf_op jit(solution)/shard_map/ppermute | solution.py:34
  48.7 14.5 %collective-permute-start.8 = (bf16[64,5248]{1,0:T(8,128)(2,1)S(1)}, bf16[64,5248]{1,0:T(8,128)(2,1)}, u32[]{:S(2)}, u32[]{:S(2)}) collective-permute-start(bf16[64,5248]{1,0:T(8,128)(2,1)S(1)} %collective-permute-done.4.refs_2_), channel_id=1, source_target_pairs={{0,48},{1,193},{2,50},{3,195},{4,52},{5,197},{6,54},{7,199},{8,56}... | collective-permute-start | bytes 2015240 | tf_op jit(solution)/shard_map/ppermute | solution.py:34
  90.8 5.7 %collective-permute-start.10 = (f32[2,8]{1,0:T(2,128)S(1)}, f32[2,8]{1,0:T(2,128)S(1)}, u32[]{:S(2)}, u32[]{:S(2)}) collective-permute-start(f32[2,8]{1,0:T(2,128)S(1)} %pad_maximum_fusion.2), channel_id=1, source_target_pairs={{0,1},{1,0},{2,3},{3,2},{4,5},{5,4},{6,7},{7,6},{8,9},{9,8},{10,11... | collective-permute-start | bytes 200 | tf_op jit(solution)/shard_map/ppermute | solution.py:34
where the time goes:
time: 97.2 us; the launch traced here: 96.9 us
  blocking collectives  42 us (43%)
  starting transfers between devices  21 us (22%)
  Pallas kernels  15.2 us (16%)
  waiting for transfers between devices  14.5 us (15%)
  other arithmetic  2.56 us (3%)
    all_to_all x3, blocking collectives, copy_for_each(): return lax.all_to_all(copies, axis, split_axis=0, concat_axis=0, tiled=True)  42 us
    ppermute x11, starting transfers between devices, moved(): return lax.ppermute(value, ALL, pairs(where))  21 us
    ppermute x11, waiting for transfers between devices, moved(): return lax.ppermute(value, ALL, pairs(where))  14.5 us
    pallas_call x1, Pallas kernels, early_stats(): pl.pallas_call(early_kernel, out_shape=(jax.ShapeDtypeStruct((8, 2 * LANE...  9.9 us
    pallas_call x1, Pallas kernels, late_stats(): pl.pallas_call(late_kernel, out_shape=jax.ShapeDtypeStruct((16, LANES), j...  5.3 us
  transfers between devices with their start and end apart: 11, of which 5 were waited for; matrix products, arithmetic and copies ran while one was open for 3% of the time, Pallas kernels for 10%

commit v1 on v0

--- a/solution.py
+++ b/solution.py
@@ -76,9 +76,7 @@
 
 
 def piece_stats(heads, pieces, order, copies=(None, None)):
-    depth = heads[0].shape[1]
-    whole = jnp.concatenate([pieces[k][start:stop, :] for k, start, stop in order], axis=0)
-    rows, notes = whole[:, :depth], whole[:, depth:]
+    rows = jnp.concatenate([pieces[k][start:stop, :] for k, start, stop in order], axis=0)
     found = []
     for head, copy in zip(heads, copies):
         if copy is not None:
@@ -101,12 +99,8 @@
         scale = jnp.exp(shift)
         norm += scale * n
         tilt += scale * (t + shift * n)
-    picks = lax.broadcasted_iota(jnp.int32, (8, LANES), 0) == lax.broadcasted_iota(jnp.int32, (8, LANES), 1)
-    marks = lax.dot_general(
-        picks.astype(jnp.bfloat16), notes, (((1,), (1,)), ((), ())), preferred_element_type=jnp.float32
-    )
     log_norm = jnp.log(norm)
-    return jnp.concatenate([peak + log_norm, log_norm - tilt / norm, marks[:6]], axis=0)
+    return jnp.concatenate([peak + log_norm, log_norm - tilt / norm, jnp.zeros((6, rows.shape[0]), jnp.float32)], axis=0)
 
 
 def early_kernel(w0, w1, *refs):
@@ -117,10 +111,10 @@
     out[...] = piece_stats((v0, v1), pieces, EARLY, copies)
 
 
-def late_kernel(place, w0, w1, early, *refs):
+def late_kernel(place, masks, ids, w0, w1, early, *refs):
     late = piece_stats((w0, w1), refs[:-1], LATE)
     out = refs[-1]
-    far, near = place[0], place[1]
+    far, near, own = place[0], place[1], place[2]
     low = lax.broadcasted_iota(jnp.int32, (8, LANES), 1) < LANES // 2
     a0, a1 = early[:, :LANES], early[:, LANES:]
     b0, b1 = late[:, :LANES], late[:, LANES:]
@@ -130,16 +124,23 @@
         value = turned[row]
         for step in range(1, 4):
             value = jnp.where(far == step, turned[(row - step) % 4], value)
-        for kind in range(4):
+        for kind in range(2):
             out[4 * kind + row : 4 * kind + row + 1, :] = value[kind : kind + 1]
+    lane = lax.broadcasted_iota(jnp.int32, (4, LANES), 1)
+    row = lax.broadcasted_iota(jnp.int32, (4, LANES), 0)
+    for kind, notes in enumerate((masks, ids)):
+        value = jnp.zeros((4, LANES), jnp.int32)
+        for k in range(4):
+            value = jnp.where((row == far) & (lane == own + k), notes[k], value)
+        out[8 + 4 * kind : 12 + 4 * kind, :] = value.astype(jnp.float32)
 
 
 def joined(parts):
-    level, spread = parts[:, :4], parts[:, 4:]
+    level, spread = parts[:, :4], parts[:, 4:8]
     top = jnp.max(level, axis=0)
     below = top[None] - level
     share = jnp.exp(-below)
-    return top, jnp.sum(share, axis=0), jnp.sum(share * (below + spread), axis=0)
+    return top, jnp.sum(share, axis=0), jnp.sum(share * (below + spread), axis=0), jnp.sum(parts[:, 8:], axis=0)
 
 
 def in_vmem(*arrays):
@@ -174,15 +175,15 @@
     )(*[pltpu.with_memory_space_constraint(h, pltpu.HBM) for h in heads], *in_vmem(*pieces))
 
 
-def late_stats(place, heads, early, pieces):
+def late_stats(places, heads, early, pieces):
     return pl.pallas_call(
         late_kernel,
         out_shape=jax.ShapeDtypeStruct((16, LANES), jnp.float32),
-        in_specs=[pl.BlockSpec(memory_space=pltpu.SMEM)] + [VMEM] * (3 + len(pieces)),
+        in_specs=[pl.BlockSpec(memory_space=pltpu.SMEM)] * 3 + [VMEM] * (3 + len(pieces)),
         out_specs=VMEM,
         cost_estimate=cost(heads),
         compiler_params=pltpu.CompilerParams(vmem_limit_bytes=12 << 20),
-    )(place, *in_vmem(*heads, early, *pieces))
+    )(*places, *in_vmem(*heads, early, *pieces))
 
 
 def per_device(hidden, unembed, loss_mask, seq_ids):
@@ -190,23 +191,22 @@
     near = jnp.where(c == 0, y, x)
     far = jnp.where(c == 0, x, y)
     heads = (unembed, moved(unembed, other_core))
-    lane = lax.broadcasted_iota(jnp.int32, (hidden.shape[0], LANES), 1)
-    notes = jnp.where(lane == 0, loss_mask[:, None], jnp.where(lane == 1, seq_ids[:, None], 0))
-    early, late = gathered(jnp.concatenate([hidden, notes.astype(hidden.dtype)], axis=1))
+    early, late = gathered(hidden)
     stats, *heads = early_stats(heads, early)
-    stats = late_stats(jnp.stack([far, near]), heads, stats, late)
+    own = near * (LANES // 4) + z * 4
+    places = (jnp.stack([far, near, own]), loss_mask, seq_ids)
+    stats = late_stats(places, heads, stats, late)
+    stats, at = lax.optimization_barrier((stats, far * LANES + own))
+    top, total, mixed, notes = joined(copy_for_each(stats, "z"))
+    log_total = jnp.log(total)
+    both = jnp.concatenate([top + log_total, log_total + mixed / total, notes], axis=0)
+    top, total, mixed, notes = joined(copy_for_each(both, ("y", "x")))
+    entropy_rows = jnp.log(total) + mixed / total
+    entropy = lax.dynamic_slice(entropy_rows.reshape(-1), (at,), (4,), allow_negative_indices=False)
     kinds = jnp.arange(SEQS, dtype=jnp.int32)[:, None, None]
-    member = (stats[8:12] > 0)[None] & (stats[12:16].astype(jnp.int32)[None] == kinds)
+    member = (notes[:4] > 0)[None] & (notes[4:].astype(jnp.int32)[None] == kinds)
     member = member.astype(jnp.float32)
     counts = jnp.sum(member, axis=(1, 2))
-    at = ((far * 4 + near) * NZ + z) * 4
-    mine, member, counts, at = lax.optimization_barrier((stats[:8], member, counts, at))
-    top, total, mixed = joined(copy_for_each(mine, "z"))
-    log_total = jnp.log(total)
-    both = jnp.concatenate([top + log_total, log_total + mixed / total], axis=0)
-    top, total, mixed = joined(copy_for_each(both, ("y", "x")))
-    entropy_rows = jnp.log(total) + mixed / total
-    entropy = lax.dynamic_slice(entropy_rows.reshape(-1), (at,), (4,), allow_negative_indices=False)
     sums = jnp.sum(member * entropy_rows[None], axis=(1, 2))
     both = jnp.stack([sums, counts])
     both = both + moved(both, other_core)

time: 97.2 us -> 96.2 us (0.990)
  other arithmetic: 2.56 us -> 0.94 us
  transfers between devices with their start and end apart: 11 -> 11, of which waited for: 5 -> 5; matrix products, arithmetic and copies ran while one was open for 3% -> 2% of each run, Pallas kernels for 10% -> 10%
where the time goes in v1:
time: 96.2 us; the launch traced here: 95.9 us
  blocking collectives  42.5 us (44%)
  starting transfers between devices  20.9 us (22%)
  Pallas kernels  15.2 us (16%)
  waiting for transfers between devices  13.9 us (14%)
  local copies, waits for them, and re-layouts  1.64 us (2%)
    all_to_all x3, blocking collectives, copy_for_each(): return lax.all_to_all(copies, axis, split_axis=0, concat_axis=0, tiled=True)  42.5 us
    ppermute x11, starting transfers between devices, moved(): return lax.ppermute(value, ALL, pairs(where))  20.9 us
    ppermute x11, waiting for transfers between devices, moved(): return lax.ppermute(value, ALL, pairs(where))  13.9 us
    pallas_call x1, Pallas kernels, early_stats(): pl.pallas_call(early_kernel, out_shape=(jax.ShapeDtypeStruct((8, 2 * LANE...  9.94 us
    pallas_call x1, Pallas kernels, late_stats(): pl.pallas_call(late_kernel, out_shape=jax.ShapeDtypeStruct((16, LANES), j...  5.3 us
  transfers between devices with their start and end apart: 11, of which 5 were waited for; matrix products, arithmetic and copies ran while one was open for 2% of the time, Pallas kernels for 10%

profile of v1, /device:TPU:1, one launch (start us, length us, event | category | flops | bytes accessed | tf_op | source)
XLA Modules:
  0.0 95.9 jit_solution(15924370542546032316)
XLA Ops:
  0.6 3.3 %collective-permute-start = (bf16[594,5120]{1,0:T(8,128)(2,1)}, bf16[594,5120]{1,0:T(8,128)(2,1)}, u32[]{:S(2)}, u32[]{:S(2)}) collective-permute-start(bf16[594,5120]{1,0:T(8,128)(2,1)} %w0.1), channel_id=1, source_target_pairs={{0,1},{1,0},{2,3},{3,2},{4,5},{5,4},{6,7},{7,6},{8,9},{9,8},{10,11... | collective-permute-start | bytes 18247688 | tf_op jit(solution)/shard_map/ppermute | solution.py:34
  3.9 0.9 broadcast_in_dim.6
  4.8 20.0 %all_to_all.15 = bf16[8,4,5120]{2,1,0:T(4,128)(2,1)S(1)} all-to-all(bf16[8,4,5120]{2,1,0:T(4,128)(2,1)S(1)} %broadcast_in_dim.6), channel_id=1, replica_groups=mesh['y'=4,'x'=4,'z'=8,'c'=2] {'z'}, dimensions={0} | all-to-all | bytes 655360 | tf_op jit(solution)/shard_map/all_to_all | solution.py:55
  24.8 0.1 reshape.27
  24.9 2.8 %collective-permute-start.2 = (bf16[32,5120]{1,0:T(8,128)(2,1)S(1)}, bf16[32,5120]{1,0:T(8,128)(2,1)S(1)}, u32[]{:S(2)}, u32[]{:S(2)}) collective-permute-start(bf16[32,5120]{1,0:T(8,128)(2,1)S(1)} %reshape.27), channel_id=1, source_target_pairs={{0,128},{1,33},{2,130},{3,35},{4,132},{5,37},{6,134},{7,39},{8,136... | collective-permute-start | bytes 983048 | tf_op jit(solution)/shard_map/ppermute | solution.py:34
  27.7 0.3 collective-permute-start.3
  28.1 2.4 %collective-permute-start.1 = (bf16[32,5120]{1,0:T(8,128)(2,1)S(1)}, bf16[32,5120]{1,0:T(8,128)(2,1)S(1)}, u32[]{:S(2)}, u32[]{:S(2)}) collective-permute-start(bf16[32,5120]{1,0:T(8,128)(2,1)S(1)} %reshape.27), channel_id=1, source_target_pairs={{0,192},{1,49},{2,194},{3,51},{4,196},{5,53},{6,198},{7,55},{8,200... | collective-permute-start | bytes 983048 | tf_op jit(solution)/shard_map/ppermute | solution.py:34
  30.4 2.3 %collective-permute-done.2 = bf16[32,5120]{1,0:T(8,128)(2,1)S(1)} collective-permute-done((bf16[32,5120]{1,0:T(8,128)(2,1)S(1)}, bf16[32,5120]{1,0:T(8,128)(2,1)S(1)}, u32[]{:S(2)}, u32[]{:S(2)}) %collective-permute-start.2) | collective-permute-done | bytes 327712 | tf_op jit(solution)/shard_map/ppermute | solution.py:34
  32.8 3.5 %collective-permute-done.3 = bf16[32,5120]{1,0:T(8,128)(2,1)S(1)} collective-permute-done((bf16[32,5120]{1,0:T(8,128)(2,1)S(1)}, bf16[32,5120]{1,0:T(8,128)(2,1)S(1)}, u32[]{:S(2)}, u32[]{:S(2)}) %collective-permute-start.3) | collective-permute-done | bytes 327712 | tf_op jit(solution)/shard_map/ppermute | solution.py:34
  36.3 1.1 %collective-permute-start.5 = (bf16[64,5120]{1,0:T(8,128)(2,1)S(1)}, bf16[64,5120]{1,0:T(8,128)(2,1)S(1)}, u32[]{:S(2)}, u32[]{:S(2)}) collective-permute-start(bf16[64,5120]{1,0:T(8,128)(2,1)S(1)} %constant_dynamic-update-slice_fusion.2.refs_1_), channel_id=1, source_target_pairs={{0,16},{1,65},{2,18},{3,67},{4,20},{5,69},{6,22},{7,71},{8,24},{9,... | collective-permute-start | bytes 1966088 | tf_op jit(solution)/shard_map/ppermute | solution.py:34
  37.3 0.0 collective-permute-done.1
  37.4 1.8 %collective-permute-start.4 = (bf16[64,5120]{1,0:T(8,128)(2,1)S(1)}, bf16[64,5120]{1,0:T(8,128)(2,1)S(1)}, u32[]{:S(2)}, u32[]{:S(2)}) collective-permute-start(bf16[64,5120]{1,0:T(8,128)(2,1)S(1)} %constant_dynamic-update-slice_fusion.refs_0_), channel_id=1, source_target_pairs={{0,48},{1,193},{2,50},{3,195},{4,52},{5,197},{6,54},{7,199},{8,56}... | collective-permute-start | bytes 1966088 | tf_op jit(solution)/shard_map/ppermute | solution.py:34
  39.2 1.4 %collective-permute-start.7 = (bf16[64,5120]{1,0:T(8,128)(2,1)S(1)}, bf16[64,5120]{1,0:T(8,128)(2,1)S(1)}, u32[]{:S(2)}, u32[]{:S(2)}) collective-permute-start(bf16[64,5120]{1,0:T(8,128)(2,1)S(1)} %constant_dynamic-update-slice_fusion.2.refs_1_), channel_id=1, source_target_pairs={{0,48},{1,193},{2,50},{3,195},{4,52},{5,197},{6,54},{7,199},{8,56}... | collective-permute-start | bytes 1966088 | tf_op jit(solution)/shard_map/ppermute | solution.py:34
  40.6 0.0 collective-permute-start.6
  40.7 6.7 %collective-permute-done.5.refs_3_ = bf16[64,5120]{1,0:T(8,128)(2,1)S(1)} collective-permute-done((bf16[64,5120]{1,0:T(8,128)(2,1)S(1)}, bf16[64,5120]{1,0:T(8,128)(2,1)S(1)}, u32[]{:S(2)}, u32[]{:S(2)}) %collective-permute-start.5) | collective-permute-done | bytes 655392 | tf_op jit(solution)/shard_map/ppermute | solution.py:34
  47.3 0.0 collective-permute-start.9
  47.3 0.0 collective-permute-done.4.refs_2_
  47.4 2.9 %collective-permute-start.8 = (bf16[64,5120]{1,0:T(8,128)(2,1)S(1)}, bf16[64,5120]{1,0:T(8,128)(2,1)}, u32[]{:S(2)}, u32[]{:S(2)}) collective-permute-start(bf16[64,5120]{1,0:T(8,128)(2,1)S(1)} %collective-permute-done.4.refs_2_), channel_id=1, source_target_pairs={{0,48},{1,193},{2,50},{3,195},{4,52},{5,197},{6,54},{7,199},{8,56}... | collective-permute-start | bytes 1966088 | tf_op jit(solution)/shard_map/ppermute | solution.py:34
  50.3 0.1 pad_add_fusion.place
  50.3 0.0 copy-start
  50.3 0.0 copy-start.1
  50.3 0.0 collective-permute-done.w1
  50.3 9.9 %shard_map.59 = (f32[8,256]{1,0:T(8,128)S(1)}, bf16[594,5120]{1,0:T(8,128)(2,1)S(1)}, bf16[594,5120]{1,0:T(8,128)(2,1)S(1)}) custom-call(bf16[594,5120]{1,0:T(8,128)(2,1)} %w0.1, bf16[594,5120]{1,0:T(8,128)(2,1)} %collective-permute-done.w1, bf16[64,5120]{1,0:T(8,128)(2,1)S(1)} %constant_dynamic-update-slice_fusion.refs_0_, ...), custom_call_target="tpu_custom_call" | custom-call | flops 3114270720 | bytes 14786560 | tf_op jit(solution)/shard_map/pallas_call | solution.py:164
  60.3 0.0 collective-permute-done.7.refs_1_
  60.3 0.0 collective-permute-done.6.refs_0_
  60.3 1.2 %collective-permute-done.9.refs_3_ = bf16[64,5120]{1,0:T(8,128)(2,1)} collective-permute-done((bf16[64,5120]{1,0:T(8,128)(2,1)S(1)}, bf16[64,5120]{1,0:T(8,128)(2,1)}, u32[]{:S(2)}, u32[]{:S(2)}) %collective-permute-start.9) | collective-permute-done | bytes 655392 | tf_op jit(solution)/shard_map/ppermute | solution.py:34
  61.5 0.0 collective-permute-done.8.refs_2_
  61.5 0.0 copy-done
  61.5 0.0 copy-done.1
  61.5 5.3 %shard_map.60 = f32[16,128]{1,0:T(8,128)S(1)} custom-call(s32[3]{0:T(128)S(1)} %pad_add_fusion.place, s32[4]{0:T(128)S(1)} %copy-done, s32[4]{0:T(128)S(1)} %copy-done.1, bf16[594,5120]{1,0:T(8,128)(2,1)S(1)} %get-tuple-element.7.w0, bf16[594,5120]{1,0:T(8,128)(2,1)S(1)} %get-tuple-element.8.w1, f32[8,256]{1,0:T(8,128)S(1)} %get-tuple-element.9.early, ...), custom_call_target="tpu_custom_call" | custom-call | flops 3114270720 | bytes 14786560 | tf_op jit(solution)/shard_map/pallas_call | solution.py:179
  66.8 9.6 %all_to_all.16 = f32[8,16,128]{2,1,0:T(8,128)S(1)} all-to-all(f32[8,16,128]{2,1,0:T(8,128)S(1)} %broadcast_in_dim.7), channel_id=1, replica_groups=mesh['y'=4,'x'=4,'z'=8,'c'=2] {'z'}, dimensions={0} | all-to-all | bytes 131072 | tf_op jit(solution)/shard_map/all_to_all | solution.py:55
  76.5 12.9 %all_to_all.17 = f32[16,16,128]{2,1,0:T(8,128)S(1)} all-to-all(f32[16,16,128]{2,1,0:T(8,128)S(1)} %broadcast_in_dim.8), channel_id=1, replica_groups=mesh['y'=4,'x'=4,'z'=8,'c'=2] {'y','x'}, dimensions={0} | all-to-all | bytes 262144 | tf_op jit(solution)/shard_map/all_to_all | solution.py:55
  89.5 0.1 select_reduce_fusion
  89.7 4.8 %collective-permute-start.10 = (f32[2,8]{1,0:T(2,128)S(1)}, f32[2,8]{1,0:T(2,128)S(1)}, u32[]{:S(2)}, u32[]{:S(2)}) collective-permute-start(f32[2,8]{1,0:T(2,128)S(1)} %pad_maximum_fusion.1), channel_id=1, source_target_pairs={{0,1},{1,0},{2,3},{3,2},{4,5},{5,4},{6,7},{7,6},{8,9},{9,8},{10,11... | collective-permute-start | bytes 200 | tf_op jit(solution)/shard_map/ppermute | solution.py:34
  94.5 0.6 dynamic_slice.3
  95.1 0.2 collective-permute-done.10
  95.4 0.5 fusion.7
  (18 shorter events, 0.3 us)
Async XLA Ops:
  0.6 49.7 %collective-permute-start = (bf16[594,5120]{1,0:T(8,128)(2,1)}, bf16[594,5120]{1,0:T(8,128)(2,1)}, u32[]{:S(2)}, u32[]{:S(2)}) collective-permute-start(bf16[594,5120]{1,0:T(8,128)(2,1)} %w0.1), channel_id=1, source_target_pairs={{0,1},{1,0},{2,3},{3,2},{4,5},{5,4},{6,7},{7,6},{8,9},{9,8},{10,11... | collective-permute-start | bytes 18247688 | tf_op jit(solution)/shard_map/ppermute | solution.py:34
  24.9 7.8 %collective-permute-start.2 = (bf16[32,5120]{1,0:T(8,128)(2,1)S(1)}, bf16[32,5120]{1,0:T(8,128)(2,1)S(1)}, u32[]{:S(2)}, u32[]{:S(2)}) collective-permute-start(bf16[32,5120]{1,0:T(8,128)(2,1)S(1)} %reshape.27), channel_id=1, source_target_pairs={{0,128},{1,33},{2,130},{3,35},{4,132},{5,37},{6,134},{7,39},{8,136... | collective-permute-start | bytes 983048 | tf_op jit(solution)/shard_map/ppermute | solution.py:34
  27.7 8.5 %collective-permute-start.3 = (bf16[32,5120]{1,0:T(8,128)(2,1)S(1)}, bf16[32,5120]{1,0:T(8,128)(2,1)S(1)}, u32[]{:S(2)}, u32[]{:S(2)}) collective-permute-start(bf16[32,5120]{1,0:T(8,128)(2,1)S(1)} %reshape.27), channel_id=1, source_target_pairs={{0,64},{1,17},{2,66},{3,19},{4,68},{5,21},{6,70},{7,23},{8,72},{9,... | collective-permute-start | bytes 983048 | tf_op jit(solution)/shard_map/ppermute | solution.py:34
  28.1 9.3 %collective-permute-start.1 = (bf16[32,5120]{1,0:T(8,128)(2,1)S(1)}, bf16[32,5120]{1,0:T(8,128)(2,1)S(1)}, u32[]{:S(2)}, u32[]{:S(2)}) collective-permute-start(bf16[32,5120]{1,0:T(8,128)(2,1)S(1)} %reshape.27), channel_id=1, source_target_pairs={{0,192},{1,49},{2,194},{3,51},{4,196},{5,53},{6,198},{7,55},{8,200... | collective-permute-start | bytes 983048 | tf_op jit(solution)/shard_map/ppermute | solution.py:34
  36.3 11.1 %collective-permute-start.5 = (bf16[64,5120]{1,0:T(8,128)(2,1)S(1)}, bf16[64,5120]{1,0:T(8,128)(2,1)S(1)}, u32[]{:S(2)}, u32[]{:S(2)}) collective-permute-start(bf16[64,5120]{1,0:T(8,128)(2,1)S(1)} %constant_dynamic-update-slice_fusion.2.refs_1_), channel_id=1, source_target_pairs={{0,16},{1,65},{2,18},{3,67},{4,20},{5,69},{6,22},{7,71},{8,24},{9,... | collective-permute-start | bytes 1966088 | tf_op jit(solution)/shard_map/ppermute | solution.py:34
  37.4 10.0 %collective-permute-start.4 = (bf16[64,5120]{1,0:T(8,128)(2,1)S(1)}, bf16[64,5120]{1,0:T(8,128)(2,1)S(1)}, u32[]{:S(2)}, u32[]{:S(2)}) collective-permute-start(bf16[64,5120]{1,0:T(8,128)(2,1)S(1)} %constant_dynamic-update-slice_fusion.refs_0_), channel_id=1, source_target_pairs={{0,48},{1,193},{2,50},{3,195},{4,52},{5,197},{6,54},{7,199},{8,56}... | collective-permute-start | bytes 1966088 | tf_op jit(solution)/shard_map/ppermute | solution.py:34
  39.2 21.1 %collective-permute-start.7 = (bf16[64,5120]{1,0:T(8,128)(2,1)S(1)}, bf16[64,5120]{1,0:T(8,128)(2,1)S(1)}, u32[]{:S(2)}, u32[]{:S(2)}) collective-permute-start(bf16[64,5120]{1,0:T(8,128)(2,1)S(1)} %constant_dynamic-update-slice_fusion.2.refs_1_), channel_id=1, source_target_pairs={{0,48},{1,193},{2,50},{3,195},{4,52},{5,197},{6,54},{7,199},{8,56}... | collective-permute-start | bytes 1966088 | tf_op jit(solution)/shard_map/ppermute | solution.py:34
  40.6 19.7 %collective-permute-start.6 = (bf16[64,5120]{1,0:T(8,128)(2,1)S(1)}, bf16[64,5120]{1,0:T(8,128)(2,1)}, u32[]{:S(2)}, u32[]{:S(2)}) collective-permute-start(bf16[64,5120]{1,0:T(8,128)(2,1)S(1)} %constant_dynamic-update-slice_fusion.refs_0_), channel_id=1, source_target_pairs={{0,16},{1,65},{2,18},{3,67},{4,20},{5,69},{6,22},{7,71},{8,24},{9,... | collective-permute-start | bytes 1966088 | tf_op jit(solution)/shard_map/ppermute | solution.py:34
  47.3 14.1 %collective-permute-start.9 = (bf16[64,5120]{1,0:T(8,128)(2,1)S(1)}, bf16[64,5120]{1,0:T(8,128)(2,1)}, u32[]{:S(2)}, u32[]{:S(2)}) collective-permute-start(bf16[64,5120]{1,0:T(8,128)(2,1)S(1)} %collective-permute-done.5.refs_3_), channel_id=1, source_target_pairs={{0,16},{1,65},{2,18},{3,67},{4,20},{5,69},{6,22},{7,71},{8,24},{9,... | collective-permute-start | bytes 1966088 | tf_op jit(solution)/shard_map/ppermute | solution.py:34
  47.4 14.1 %collective-permute-start.8 = (bf16[64,5120]{1,0:T(8,128)(2,1)S(1)}, bf16[64,5120]{1,0:T(8,128)(2,1)}, u32[]{:S(2)}, u32[]{:S(2)}) collective-permute-start(bf16[64,5120]{1,0:T(8,128)(2,1)S(1)} %collective-permute-done.4.refs_2_), channel_id=1, source_target_pairs={{0,48},{1,193},{2,50},{3,195},{4,52},{5,197},{6,54},{7,199},{8,56}... | collective-permute-start | bytes 1966088 | tf_op jit(solution)/shard_map/ppermute | solution.py:34
  50.3 11.2 %copy-start = (s32[4]{0:T(128)S(1)}, s32[4]{0:T(128)}, u32[]{:S(2)}) copy-start(s32[4]{0:T(128)} %masks.1) | copy-start | bytes 52
  50.3 11.2 %copy-start.1 = (s32[4]{0:T(128)S(1)}, s32[4]{0:T(128)}, u32[]{:S(2)}) copy-start(s32[4]{0:T(128)} %ids.1) | copy-start | bytes 52
  89.7 5.7 %collective-permute-start.10 = (f32[2,8]{1,0:T(2,128)S(1)}, f32[2,8]{1,0:T(2,128)S(1)}, u32[]{:S(2)}, u32[]{:S(2)}) collective-permute-start(f32[2,8]{1,0:T(2,128)S(1)} %pad_maximum_fusion.1), channel_id=1, source_target_pairs={{0,1},{1,0},{2,3},{3,2},{4,5},{5,4},{6,7},{7,6},{8,9},{9,8},{10,11... | collective-permute-start | bytes 200 | tf_op jit(solution)/shard_map/ppermute | solution.py:34
